TPU v7x, 32 devices: a 4x4x1 block of a 4x4x8 slice. The times are simulated.
32 devices in a mesh: dp: 2 (over z, core), tp: 16 (over x, y).
Axes of the slice: x: 4, y: 4, z: 1, core: 2. Of those that a mesh axis runs over, the one named last changes fastest.
The devices are a block of a 4x4x8 slice.
Arguments:
- x: bfloat16 [4096, 3584], P('dp'), parts along dimension 0
- dy: bfloat16 [4096, 3584], P('dp'), parts along dimension 0
- gate: bfloat16 [4096, 14336], P('dp', 'tp'), parts along dimension 0
- up: bfloat16 [4096, 14336], P('dp', 'tp'), parts along dimension 0
- w_gate: bfloat16 [3584, 14336], P(None, 'tp')
- w_up: bfloat16 [3584, 14336], P(None, 'tp')
- w_down: bfloat16 [14336, 3584], P('tp')
Outputs:
- output 1: bfloat16 [4096, 3584], P('dp'), parts along dimension 0
- output 2: bfloat16 [7168, 14336], P('dp', 'tp'), parts along dimension 0
- output 3: bfloat16 [7168, 14336], P('dp', 'tp'), parts along dimension 0
- output 4: bfloat16 [28672, 3584], P(('dp', 'tp')), parts along dimension 0
There are 2 independent parts. A program takes and returns all parts, laid end to end along the dimension named above; an argument that names none is the same for every part.
All inputs are finite; a program needn't handle non-finite values.
Results may differ from a plain program's by a relative error of at most 0.012.
Values are sent between devices in bfloat16 or wider.
A program may use at most 768 MiB of HBM per device.

v0:
```python
import jax
import jax.numpy as jnp
from jax import lax
from jax.sharding import PartitionSpec as P


def act(gate, up):
    return jax.nn.gelu(gate) * up


def solution(mesh):
    def step(x, dy, gate, up, w_gate, w_up, w_down):
        hidden, back = jax.vjp(act, gate.astype(jnp.float32), up.astype(jnp.float32))
        d_hidden = jnp.dot(dy, w_down.T, preferred_element_type=jnp.float32)
        d_gate, d_up = (g.astype(jnp.bfloat16) for g in back(d_hidden))
        term = jnp.dot(d_gate, w_gate.T, preferred_element_type=jnp.float32) + jnp.dot(d_up, w_up.T, preferred_element_type=jnp.float32)
        dx = lax.psum(term.astype(jnp.bfloat16), "tp")
        dw_gate = jnp.dot(x.T, d_gate, preferred_element_type=jnp.float32)
        dw_up = jnp.dot(x.T, d_up, preferred_element_type=jnp.float32)
        dw_down = jnp.dot(hidden.astype(jnp.bfloat16).T, dy, preferred_element_type=jnp.float32)
        return dx, *(g.astype(jnp.bfloat16) for g in (dw_gate, dw_up, dw_down))

    tokens, columns, rows = P("dp", None), P(None, "tp"), P("tp", None)
    return jax.shard_map(
        step,
        mesh=mesh,
        in_specs=(tokens, tokens, P("dp", "tp"), P("dp", "tp"), columns, columns, rows),
        out_specs=(tokens, P("dp", "tp"), P("dp", "tp"), P(("dp", "tp"), None)),
        check_vma=False,
    )
```

profile of v0, /device:TPU:96, one launch (start us, length us, event | category | flops | bytes accessed | tf_op | source)
XLA Modules:
  0.0 289.0 jit_solution(16565889117884642288)
XLA Ops:
  7.2 0.1 all-reduce.2.cloned.1.call-start
  7.2 0.0 copy-start
  7.3 25.9 %fusion.4 = (bf16[2048,896]{1,0:T(8,128)(2,1)S(1)}, f32[2048,896]{1,0:T(8,128)}) fusion(bf16[2048,896]{1,0:T(8,128)(2,1)} %param.9, bf16[2048,896]{1,0:T(8,128)(2,1)} %param.10, bf16[2048,3584]{1,0:T(8,128)(2,1)} %param.8, bf16[896,3584]{1,0:T(8,128)(2,1)} %param.13), kind=kOutput, calls=%fused_computation.12 | convolution fusion | flops 13195542528 | bytes 39452672 | tf_op jit(solution)/shard_map/dot_general | solution.py:14
  33.1 0.0 copy-start.1
  33.1 0.0 copy-done
  33.2 19.0 %fusion.21 = f32[2048,3584]{1,0:T(8,128)} fusion(bf16[2048,896]{1,0:T(8,128)(2,1)S(1)} %get-tuple-element.8, bf16[3584,896]{1,0:T(8,128)(2,1)S(1)} %copy-done), kind=kOutput, calls=%fused_computation.32 | convolution fusion | flops 13153337344 | bytes 39452672 | tf_op jit(solution)/shard_map/dot_general | solution.py:16
  52.2 0.0 copy-done.1
  52.2 25.9 %add_convert_fusion = bf16[2048,3584]{1,0:T(8,128)(2,1)} fusion(f32[2048,3584]{1,0:T(8,128)} %fusion.21, bf16[3584,896]{1,0:T(8,128)(2,1)} %param.12, f32[2048,896]{1,0:T(8,128)} %get-tuple-element.9, bf16[2048,896]{1,0:T(8,128)(2,1)} %param.9), kind=kOutput, calls=%fused_computation | convolution fusion | flops 13188202496 | bytes 61472768 | tf_op jit(solution)/shard_map/dot_general | solution.py:16
  78.0 0.1 all-reduce.2.cloned.1.call-update
  78.1 19.9 %fusion.10 = bf16[3584,896]{0,1:T(8,128)(2,1)} fusion(bf16[2048,896]{1,0:T(8,128)(2,1)} %copy-done.1, bf16[2048,3584]{1,0:T(8,128)(2,1)} %param.7), kind=kOutput, calls=%fused_computation.22 | convolution fusion | flops 13156548608 | bytes 24772608 | tf_op jit(solution)/shard_map/dot_general | solution.py:18
  98.0 9.6 %copy.11 = bf16[3584,896]{1,0:T(8,128)(2,1)} copy(bf16[3584,896]{0,1:T(8,128)(2,1)} %fusion.10) | data formatting | bytes 12845056
  107.5 25.1 %fusion.11 = bf16[3584,896]{0,1:T(8,128)(2,1)} fusion(bf16[2048,3584]{1,0:T(8,128)(2,1)} %param.7, f32[2048,896]{1,0:T(8,128)} %get-tuple-element.9, bf16[2048,896]{1,0:T(8,128)(2,1)} %param.9), kind=kOutput, calls=%fused_computation.23 | convolution fusion | flops 13176733696 | bytes 32112640 | tf_op jit(solution)/shard_map/dot_general | solution.py:19
  132.6 9.6 %copy.12 = bf16[3584,896]{1,0:T(8,128)(2,1)} copy(bf16[3584,896]{0,1:T(8,128)(2,1)} %fusion.11) | data formatting | bytes 12845056
  142.2 24.5 %convolution_convert_fusion = bf16[896,3584]{1,0:T(8,128)(2,1)} fusion(bf16[2048,3584]{1,0:T(8,128)(2,1)} %param.8, bf16[2048,896]{1,0:T(8,128)(2,1)} %param.10, bf16[2048,896]{1,0:T(8,128)(2,1)} %param.9), kind=kOutput, calls=%fused_computation.19 | convolution fusion | flops 13178568704 | bytes 28442624 | tf_op jit(solution)/shard_map/dot_general | solution.py:20
  166.7 102.3 %all-reduce.2.cloned.1.call-done = bf16[2048,3584]{1,0:T(8,128)(2,1)} async-done(((bf16[2048,3584]{1,0:T(8,128)(2,1)}), bf16[2048,3584]{1,0:T(8,128)(2,1)}) %all-reduce.2.cloned.1.call-update) | async-done | bytes 14680080 | tf_op jit(solution)/shard_map/psum | solution.py:17
  269.0 13.1 %copy.14 = bf16[2048,3584]{1,0:T(8,128)(2,1)} copy(bf16[2048,3584]{1,0:T(8,128)(2,1)} %all-reduce.2.cloned.1.call-done) | data formatting | bytes 29360128
Async XLA Ops:
  7.2 261.8 %all-reduce.2.cloned.1.call-start = ((), (), s32[]{:S(2)}) async-start(), calls=%async_computation | async-start | bytes 29360128 | tf_op jit(solution)/shard_map/psum | solution.py:17
  7.2 25.9 %copy-start = (bf16[3584,896]{1,0:T(8,128)(2,1)S(1)}, bf16[3584,896]{1,0:T(8,128)(2,1)}, u32[]{:S(2)}) copy-start(bf16[3584,896]{1,0:T(8,128)(2,1)} %param.11) | copy-start | bytes 19267588
  33.1 19.0 %copy-start.1 = (bf16[2048,896]{1,0:T(8,128)(2,1)}, bf16[2048,896]{1,0:T(8,128)(2,1)S(1)}, u32[]{:S(2)}) copy-start(bf16[2048,896]{1,0:T(8,128)(2,1)S(1)} %get-tuple-element.8) | copy-start | bytes 11010052
Sparse Core Ops, SparseCore 0:
  78.2 190.7 all-reduce.1
where the time goes:
time: 291 us; the launch traced here: 289 us
  matrix products  140 us (48%)
  waiting for transfers between devices  102 us (35%)
  local copies, waits for them, and re-layouts  32.2 us (11%)
  between operations  14.1 us (5%)
    psum x1, waiting for transfers between devices, step(): dx = lax.psum(term.astype(jnp.bfloat16), 'tp')  102 us
    unnamed x7, local copies, waits for them, and re-layouts  32.2 us
    dot_general x1, matrix products, step(): d_hidden = jnp.dot(dy, w_down.T, preferred_element_type=jnp.float32)  25.9 us
    dot_general x1, matrix products, step(): jnp.dot(d_up, w_up.T, preferred_element_type=jnp.float32)  25.9 us
    dot_general x1, matrix products, step(): dw_up = jnp.dot(x.T, d_up, preferred_element_type=jnp.float32)  25.1 us
    dot_general x1, matrix products, step(): jnp.dot(hidden.astype(jnp.bfloat16).T, dy, preferred_element_type=jnp.flo...  24.5 us
    dot_general x1, matrix products, step(): dw_gate = jnp.dot(x.T, d_gate, preferred_element_type=jnp.float32)  19.9 us
    dot_general x1, matrix products, step(): jnp.dot(d_gate, w_gate.T, preferred_element_type=jnp.float32)  19 us
  transfers between devices with their start and end apart: 1, of which 1 were waited for; matrix products, arithmetic and copies ran while one was open for 31% of the time, Pallas kernels for 0%

commit v1 on v0

v1 whole, which is shorter than its diff:
```python
import functools
import math

import jax
import jax.numpy as jnp
from jax import lax
from jax.experimental import pallas as pl
from jax.experimental.pallas import tpu as pltpu
from jax.sharding import PartitionSpec as P

MESH = pl.DeviceIdType.MESH
F32 = jnp.float32
BF16 = jnp.bfloat16
LAST = (((1,), (1,)), ((), ()))

BLOCK = 256
SLAB = 256
ACT_ROWS = 32
HOPS = 3


def act(gate, up):
    return jax.nn.gelu(gate) * up


def kernel(
    side, x, dy, gate, up, w_gate, w_up, w_down,
    dx, dw_gate, dw_up, dw_down,
    wgu, wd, dgu, hid_t, dyb, gb, ub, dh, hb, term, acc, st1, rv1, st2, rv2, fin,
    xb, xt, yb, og, ou, od,
    in_sem, w_sem, s1_send, s2_send, r1_recv, r2_recv, ag_send, ag_recv, fin_sem,
    xy_sem, o_sem,
):
    rows, d = dx.shape
    ff = w_down.shape[0]
    blocks = rows // BLOCK
    part = BLOCK // side
    sub = part // side
    quarter = d // 4
    slabs = d // SLAB

    me = lax.axis_index("tp")
    px, py = me // side, me % side

    def device(axis, sign):
        if axis == 0:
            return {"tp": (px + side + sign) % side * side + py}
        return {"tp": px * side + (py + side + sign) % side}

    flows = ((0, 1, 1), (0, 1, -1), (1, 0, 1), (1, 0, -1))
    pos = (px, py)

    def cols(c):
        return pl.ds(c * quarter, quarter)

    def load_block(t, slot):
        r = pl.ds(pl.multiple_of(t * BLOCK, BLOCK), BLOCK)
        return (
            pltpu.make_async_copy(dy.at[r, :], dyb.at[slot], in_sem.at[slot, 0]),
            pltpu.make_async_copy(gate.at[r, :], gb.at[slot], in_sem.at[slot, 1]),
            pltpu.make_async_copy(up.at[r, :], ub.at[slot], in_sem.at[slot, 2]),
        )

    load_wd = pltpu.make_async_copy(w_down, wd, w_sem.at[0])
    load_wg = pltpu.make_async_copy(w_gate, wgu.at[:, pl.ds(0, ff)], w_sem.at[1])
    load_wu = pltpu.make_async_copy(w_up, wgu.at[:, pl.ds(ff, ff)], w_sem.at[2])

    load_wd.start()
    for copy in load_block(0, 0):
        copy.start()
    load_wg.start()
    load_wu.start()

    barrier = pltpu.get_barrier_semaphore()
    for axis in (0, 1):
        for sign in (1, -1):
            pl.semaphore_signal(barrier, inc=1, device_id=device(axis, sign), device_id_type=MESH)
    pl.semaphore_wait(barrier, 4)

    def hop(h, c, b):
        a1, a2, sign = flows[c]
        slot = b % 2
        if h < HOPS:
            return pltpu.make_async_remote_copy(
                st1.at[h, c], rv1.at[slot, h, c], s1_send.at[h, c], r1_recv.at[slot, h, c],
                device_id=device(a1, sign), device_id_type=MESH,
            )
        if h < 2 * HOPS:
            s = h - HOPS
            return pltpu.make_async_remote_copy(
                st2.at[s, c], rv2.at[slot, s, c], s2_send.at[s, c], r2_recv.at[slot, s, c],
                device_id=device(a2, sign), device_id_type=MESH,
            )
        s = h - 2 * HOPS
        p1, p2 = pos[a1], pos[a2]
        if s < HOPS:
            q = (p2 + side - sign * s) % side
            r = pl.ds(pl.multiple_of(b * BLOCK + p1 * part + q * sub, sub), sub)
            to = device(a2, sign)
        else:
            q = (p1 + side - sign * (s - HOPS)) % side
            r = pl.ds(pl.multiple_of(b * BLOCK + q * part, part), part)
            to = device(a1, sign)
        where = dx.at[r, cols(c)]
        return pltpu.make_async_remote_copy(
            fin.at[c] if s == 0 else where, where, ag_send.at[s, c], ag_recv.at[slot, s, c],
            device_id=to, device_id_type=MESH,
        )

    def own_piece(c, b):
        a1, a2, sign = flows[c]
        r = pl.ds(pl.multiple_of(b * BLOCK + pos[a1] * part + pos[a2] * sub, sub), sub)
        return pltpu.make_async_copy(fin.at[c], dx.at[r, cols(c)], fin_sem.at[c])

    def term_part(b, c, q):
        r = pl.ds(pl.multiple_of(q * part, part), part)
        return term[b % 3, r, cols(c)]

    def stage(h, b):
        for c in range(4):
            a1, a2, sign = flows[c]
            p1, p2 = pos[a1], pos[a2]
            if h > 0:
                hop(h - 1, c, b).wait_recv()
            if h < HOPS:
                q = (p1 + 2 * side - sign * (1 + h)) % side
                value = term_part(b, c, q)
                if h > 0:
                    value = value + rv1[b % 2, h - 1, c].astype(F32)
                st1[h, c] = value.astype(BF16)
            elif h < 2 * HOPS:
                s = h - HOPS
                if s == 0:
                    acc[b % 3, c] = term_part(b, c, p1) + rv1[b % 2, HOPS - 1, c].astype(F32)
                q = (p2 + 2 * side - sign * (1 + s)) % side
                value = acc[b % 3, c, pl.ds(pl.multiple_of(q * sub, sub), sub), :]
                if s > 0:
                    value = value + rv2[b % 2, s - 1, c].astype(F32)
                st2[s, c] = value.astype(BF16)
            elif h == 2 * HOPS:
                value = acc[b % 3, c, pl.ds(pl.multiple_of(p2 * sub, sub), sub), :]
                fin[c] = (value + rv2[b % 2, HOPS - 1, c].astype(F32)).astype(BF16)
                own_piece(c, b).start()
            elif h == 2 * HOPS + 1:
                own_piece(c, b).wait()
            if h < 4 * HOPS:
                hop(h, c, b).start()

    def compute(t):
        slot = t % 2
        for copy in load_block(t, slot):
            copy.wait()

        @pl.when(t + 1 < blocks)
        def _():
            for copy in load_block(t + 1, 1 - slot):
                copy.start()

        @pl.when(t == 0)
        def _():
            load_wd.wait()

        dh[...] = lax.dot_general(dyb[slot], wd[...], LAST, preferred_element_type=F32)
        base = pl.multiple_of(t * BLOCK, BLOCK)

        @pl.loop(0, BLOCK // ACT_ROWS)
        def _(i):
            r = pl.ds(pl.multiple_of(i * ACT_ROWS, ACT_ROWS), ACT_ROWS)
            g = pl.ds(pl.multiple_of(base + i * ACT_ROWS, ACT_ROWS), ACT_ROWS)
            hidden, back = jax.vjp(act, gb[slot, r, :].astype(F32), ub[slot, r, :].astype(F32))
            d_gate, d_up = back(dh[r, :])
            dgu[g, pl.ds(0, ff)] = d_gate.astype(BF16)
            dgu[g, pl.ds(ff, ff)] = d_up.astype(BF16)
            hb[r, :] = hidden.astype(BF16)

        hid_t[:, pl.ds(base, BLOCK)] = hb[...].T

        @pl.when(t == 0)
        def _():
            load_wg.wait()
            load_wu.wait()

        lhs = dgu[pl.ds(base, BLOCK), :]
        wide = d // 7

        @pl.loop(0, 7)
        def _(i):
            n = pl.ds(pl.multiple_of(i * wide, wide), wide)
            term[t % 3, :, n] = lax.dot_general(lhs, wgu[n, :], LAST, preferred_element_type=F32)

    def load_slab(j, slot):
        n = pl.ds(pl.multiple_of(j * SLAB, SLAB), SLAB)
        return (
            pltpu.make_async_copy(x.at[:, n], xb.at[slot], xy_sem.at[slot, 0]),
            pltpu.make_async_copy(dy.at[:, n], yb.at[slot], xy_sem.at[slot, 1]),
        )

    def store_slab(j, slot):
        n = pl.ds(pl.multiple_of(j * SLAB, SLAB), SLAB)
        return (
            pltpu.make_async_copy(og.at[slot], dw_gate.at[n, :], o_sem.at[slot, 0]),
            pltpu.make_async_copy(ou.at[slot], dw_up.at[n, :], o_sem.at[slot, 1]),
            pltpu.make_async_copy(od.at[slot], dw_down.at[:, n], o_sem.at[slot, 2]),
        )

    def weights(j):
        slot = j % 2
        for copy in load_slab(j, slot):
            copy.wait()

        @pl.when(j >= 2)
        def _():
            for copy in store_slab(j - 2, slot):
                copy.wait()

        xt[...] = xb[slot].T
        og[slot] = jnp.dot(xt[...], dgu[:, pl.ds(0, ff)], preferred_element_type=F32).astype(BF16)
        ou[slot] = jnp.dot(xt[...], dgu[:, pl.ds(ff, ff)], preferred_element_type=F32).astype(BF16)
        od[slot] = jnp.dot(hid_t[...], yb[slot], preferred_element_type=F32).astype(BF16)
        for copy in store_slab(j, slot):
            copy.start()

        @pl.when(j + 2 < slabs)
        def _():
            for copy in load_slab(j + 2, slot):
                copy.start()

    @pl.loop(0, blocks + 4 * HOPS + 1)
    def _(t):
        for h in range(4 * HOPS, 0, -1):
            b = t - h
            if h < 4 * HOPS:
                @pl.when((b >= 1) & (b <= blocks))
                def _():
                    for c in range(4):
                        hop(h, c, b - 1).wait_send()

            @pl.when((b >= 0) & (b < blocks))
            def _():
                stage(h, b)

        @pl.when((t >= 1) & (t <= blocks))
        def _():
            for c in range(4):
                hop(0, c, t - 1).wait_send()

        @pl.when(t < blocks)
        def _():
            compute(t)
            stage(0, t)

        @pl.when(t == blocks - 1)
        def _():
            for j in range(2):
                for copy in load_slab(j, j):
                    copy.start()

        first = (t - blocks) * 2

        @pl.when((t >= blocks) & (first < slabs))
        def _():
            @pl.loop(0, 2)
            def _(i):
                weights(first + i)

    for j in range(slabs - 2, slabs):
        for copy in store_slab(j, j % 2):
            copy.wait()


def solution(mesh):
    n = mesh.shape["tp"]
    side = math.isqrt(n)

    def step(x, dy, gate, up, w_gate, w_up, w_down):
        rows, d = x.shape
        ff = w_down.shape[0]
        part = BLOCK // side
        sub = part // side
        quarter = d // 4
        hbm = pl.BlockSpec(memory_space=pl.ANY)
        dma = pltpu.SemaphoreType.DMA
        return pl.pallas_call(
            functools.partial(kernel, side),
            out_shape=(
                jax.ShapeDtypeStruct((rows, d), BF16),
                jax.ShapeDtypeStruct((d, ff), BF16),
                jax.ShapeDtypeStruct((d, ff), BF16),
                jax.ShapeDtypeStruct((ff, d), BF16),
            ),
            in_specs=[hbm] * 7,
            out_specs=(hbm,) * 4,
            scratch_shapes=[
                pltpu.VMEM((d, 2 * ff), BF16),
                pltpu.VMEM((ff, d), BF16),
                pltpu.VMEM((rows, 2 * ff), BF16),
                pltpu.VMEM((ff, rows), BF16),
                pltpu.VMEM((2, BLOCK, d), BF16),
                pltpu.VMEM((2, BLOCK, ff), BF16),
                pltpu.VMEM((2, BLOCK, ff), BF16),
                pltpu.VMEM((BLOCK, ff), F32),
                pltpu.VMEM((BLOCK, ff), BF16),
                pltpu.VMEM((3, BLOCK, d), F32),
                pltpu.VMEM((3, 4, part, quarter), F32),
                pltpu.VMEM((HOPS, 4, part, quarter), BF16),
                pltpu.VMEM((2, HOPS, 4, part, quarter), BF16),
                pltpu.VMEM((HOPS, 4, sub, quarter), BF16),
                pltpu.VMEM((2, HOPS, 4, sub, quarter), BF16),
                pltpu.VMEM((4, sub, quarter), BF16),
                pltpu.VMEM((2, rows, SLAB), BF16),
                pltpu.VMEM((SLAB, rows), BF16),
                pltpu.VMEM((2, rows, SLAB), BF16),
                pltpu.VMEM((2, SLAB, ff), BF16),
                pltpu.VMEM((2, SLAB, ff), BF16),
                pltpu.VMEM((2, ff, SLAB), BF16),
                dma((2, 3)),
                dma((3,)),
                dma((HOPS, 4)),
                dma((HOPS, 4)),
                dma((2, HOPS, 4)),
                dma((2, HOPS, 4)),
                dma((2 * HOPS, 4)),
                dma((2, 2 * HOPS, 4)),
                dma((4,)),
                dma((2, 2)),
                dma((2, 3)),
            ],
            compiler_params=pltpu.CompilerParams(
                collective_id=0, has_side_effects=True, vmem_limit_bytes=67043328
            ),
        )(x, dy, gate, up, w_gate, w_up, w_down)

    tokens, columns, rows = P("dp", None), P(None, "tp"), P("tp", None)
    return jax.shard_map(
        step,
        mesh=mesh,
        in_specs=(tokens, tokens, P("dp", "tp"), P("dp", "tp"), columns, columns, rows),
        out_specs=(tokens, P("dp", "tp"), P("dp", "tp"), P(("dp", "tp"), None)),
        check_vma=False,
    )
```

time: 291 us -> 230 us (0.79)
  Pallas kernels: 0 us -> 202 us
  matrix products: 140 us -> 0 us
  waiting for transfers between devices: 102 us -> 0 us
  between operations: 14.1 us -> 0.65 us
  local copies, waits for them, and re-layouts: 32.2 us -> 27.2 us
    pallas_call x0 -> x1, Pallas kernels: none -> 202 us  [step(): pl.pallas_call(functools.partial(kernel, side), out_shape=(jax.ShapeDtype...]
    dot_general x6 -> x0, matrix products: 140 us -> none  [the longest x1 25.9 us: step(): d_hidden = jnp.dot(dy, w_down.T, preferred_element_type=jnp.float32)]
    psum x1 -> x0, waiting for transfers between devices: 102 us -> none  [step(): dx = lax.psum(term.astype(jnp.bfloat16), 'tp')]
    unnamed x7 -> x10, local copies, waits for them, and re-layouts: 32.2 us -> 27.2 us
  transfers between devices with their start and end apart: 1 -> 0, of which waited for: 1 -> 0; matrix products, arithmetic and copies ran while one was open for 31% -> 0% of each run, Pallas kernels for 0% -> 0%
where the time goes in v1:
time: 230 us
  Pallas kernels  202 us (88%)
  local copies, waits for them, and re-layouts  27.2 us (12%)
    pallas_call x1, Pallas kernels, step(): pl.pallas_call(functools.partial(kernel, side), out_shape=(jax.ShapeDtype...  202 us
    unnamed x10, local copies, waits for them, and re-layouts  27.2 us

profile of v1, /device:TPU:96, one launch (start us, length us, event | category | flops | bytes accessed | tf_op | source)
XLA Modules:
  0.0 229.8 jit_solution(16169475456541693399)
XLA Ops:
  0.6 202.0 %shard_map.102 = (bf16[2048,3584]{1,0:T(8,128)(2,1)}, bf16[3584,896]{1,0:T(8,128)(2,1)}, bf16[3584,896]{1,0:T(8,128)(2,1)}, bf16[896,3584]{1,0:T(8,128)(2,1)}) custom-call(bf16[2048,3584]{1,0:T(8,128)(2,1)} %x.1, bf16[2048,3584]{1,0:T(8,128)(2,1)} %dy.1, bf16[2048,896]{1,0:T(8,128)(2,1)} %gate.1, bf16[2048,896]{1,0:T(8,128)(2,1)} %up.1, ...), custom_call_target="tpu_custom_call" | custom-call | tf_op jit(solution)/shard_map/pallas_call | solution.py:283
  202.6 13.1 %copy.15 = bf16[2048,3584]{1,0:T(8,128)(2,1)} copy(bf16[2048,3584]{1,0:T(8,128)(2,1)} %get-tuple-element.8) | data formatting | bytes 29360128
  215.7 0.0 copy-start
  215.7 0.0 slice-start
  215.7 6.7 %copy.16 = bf16[3584,896]{1,0:T(8,128)(2,1)} copy(bf16[3584,896]{1,0:T(8,128)(2,1)} %get-tuple-element.9) | data formatting | bytes 12845056
  222.5 0.0 copy-done
  222.5 0.0 slice-start.1
  222.5 3.3 %copy.17 = bf16[3584,896]{1,0:T(8,128)(2,1)} copy(bf16[3584,896]{1,0:T(8,128)(2,1)S(1)} %copy-done) | data formatting | bytes 12845056
  225.7 0.0 slice-done
  225.7 1.3 slice-done.1
  227.0 2.7 %copy.18 = bf16[896,3584]{1,0:T(8,128)(2,1)} copy(bf16[896,3584]{1,0:T(8,128)(2,1)S(1)} %bitcast.1) | data formatting | bytes 12845056
  (1 shorter events, 0.0 us)
Async XLA Ops:
  215.7 6.8 %copy-start = (bf16[3584,896]{1,0:T(8,128)(2,1)S(1)}, bf16[3584,896]{1,0:T(8,128)(2,1)}, u32[]{:S(2)}) copy-start(bf16[3584,896]{1,0:T(8,128)(2,1)} %get-tuple-element.10) | copy-start | bytes 19267588
  215.7 10.0 %slice-start = ((s8[6422528]{0:T(1024)(128)(4,1)}), s8[4194304]{0:T(1024)(128)(4,1)S(1)}, s32[]{:S(2)}) async-start(s8[6422528]{0:T(1024)(128)(4,1)} %bitcast), calls=%async_computation | async-start | bytes 8388608
  222.5 4.6 %slice-start.1 = ((s8[6422528]{0:T(1024)(128)(4,1)}), s8[2228224]{0:T(1024)(128)(4,1)S(1)}, s32[]{:S(2)}) async-start(s8[6422528]{0:T(1024)(128)(4,1)} %bitcast), calls=%async_computation.1 | async-start | bytes 4456448

commit v2 on v1

--- a/solution.py
+++ b/solution.py
@@ -25,11 +25,9 @@
 
 def kernel(
     side, x, dy, gate, up, w_gate, w_up, w_down,
-    dx, dw_gate, dw_up, dw_down,
-    wgu, wd, dgu, hid_t, dyb, gb, ub, dh, hb, term, acc, st1, rv1, st2, rv2, fin,
-    xb, xt, yb, og, ou, od,
-    in_sem, w_sem, s1_send, s2_send, r1_recv, r2_recv, ag_send, ag_recv, fin_sem,
-    xy_sem, o_sem,
+    dx, wgu, wd,
+    dgu, hid_t, dyb, gb, ub, dh, hb, term, acc, st1, rv1, st2, rv2, fin, xb, xt, yb,
+    in_sem, w_sem, s1_send, s2_send, r1_recv, r2_recv, ag_send, ag_recv, fin_sem, xy_sem,
 ):
     rows, d = dx.shape
     ff = w_down.shape[0]
@@ -116,8 +114,8 @@
         r = pl.ds(pl.multiple_of(q * part, part), part)
         return term[b % 3, r, cols(c)]
 
-    def stage(h, b):
-        for c in range(4):
+    def stage(h, b, which=range(4)):
+        for c in which:
             a1, a2, sign = flows[c]
             p1, p2 = pos[a1], pos[a2]
             if h > 0:
@@ -146,7 +144,7 @@
             if h < 4 * HOPS:
                 hop(h, c, b).start()
 
-    def compute(t):
+    def front(t):
         slot = t % 2
         for copy in load_block(t, slot):
             copy.wait()
@@ -175,18 +173,10 @@
 
         hid_t[:, pl.ds(base, BLOCK)] = hb[...].T
 
-        @pl.when(t == 0)
-        def _():
-            load_wg.wait()
-            load_wu.wait()
-
-        lhs = dgu[pl.ds(base, BLOCK), :]
-        wide = d // 7
-
-        @pl.loop(0, 7)
-        def _(i):
-            n = pl.ds(pl.multiple_of(i * wide, wide), wide)
-            term[t % 3, :, n] = lax.dot_general(lhs, wgu[n, :], LAST, preferred_element_type=F32)
+    def back_half(t, i):
+        lhs = dgu[pl.ds(pl.multiple_of(t * BLOCK, BLOCK), BLOCK), :]
+        n = pl.ds(i * (d // 2), d // 2)
+        term[t % 3, :, n] = lax.dot_general(lhs, wgu[n, :], LAST, preferred_element_type=F32)
 
     def load_slab(j, slot):
         n = pl.ds(pl.multiple_of(j * SLAB, SLAB), SLAB)
@@ -195,30 +185,17 @@
             pltpu.make_async_copy(dy.at[:, n], yb.at[slot], xy_sem.at[slot, 1]),
         )
 
-    def store_slab(j, slot):
-        n = pl.ds(pl.multiple_of(j * SLAB, SLAB), SLAB)
-        return (
-            pltpu.make_async_copy(og.at[slot], dw_gate.at[n, :], o_sem.at[slot, 0]),
-            pltpu.make_async_copy(ou.at[slot], dw_up.at[n, :], o_sem.at[slot, 1]),
-            pltpu.make_async_copy(od.at[slot], dw_down.at[:, n], o_sem.at[slot, 2]),
-        )
-
     def weights(j):
         slot = j % 2
         for copy in load_slab(j, slot):
             copy.wait()
 
-        @pl.when(j >= 2)
-        def _():
-            for copy in store_slab(j - 2, slot):
-                copy.wait()
-
+        n = pl.ds(pl.multiple_of(j * SLAB, SLAB), SLAB)
         xt[...] = xb[slot].T
-        og[slot] = jnp.dot(xt[...], dgu[:, pl.ds(0, ff)], preferred_element_type=F32).astype(BF16)
-        ou[slot] = jnp.dot(xt[...], dgu[:, pl.ds(ff, ff)], preferred_element_type=F32).astype(BF16)
-        od[slot] = jnp.dot(hid_t[...], yb[slot], preferred_element_type=F32).astype(BF16)
-        for copy in store_slab(j, slot):
-            copy.start()
+        for i in range(2):
+            f = pl.ds(i * ff, ff)
+            wgu[n, f] = jnp.dot(xt[...], dgu[:, f], preferred_element_type=F32).astype(BF16)
+        wd[:, n] = jnp.dot(hid_t[...], yb[slot], preferred_element_type=F32).astype(BF16)
 
         @pl.when(j + 2 < slabs)
         def _():
@@ -227,27 +204,44 @@
 
     @pl.loop(0, blocks + 4 * HOPS + 1)
     def _(t):
-        for h in range(4 * HOPS, 0, -1):
-            b = t - h
-            if h < 4 * HOPS:
-                @pl.when((b >= 1) & (b <= blocks))
-                def _():
-                    for c in range(4):
-                        hop(h, c, b - 1).wait_send()
-
-            @pl.when((b >= 0) & (b < blocks))
-            def _():
-                stage(h, b)
-
-        @pl.when((t >= 1) & (t <= blocks))
-        def _():
-            for c in range(4):
-                hop(0, c, t - 1).wait_send()
+        def events(*hops):
+            for h in hops:
+                b = t - h
+                if h < 4 * HOPS:
+                    @pl.when((b >= 1) & (b <= blocks))
+                    def _():
+                        for c in range(4):
+                            hop(h, c, b - 1).wait_send()
+
+                if h > 0:
+                    @pl.when((b >= 0) & (b < blocks))
+                    def _():
+                        stage(h, b)
+
+        events(*range(4 * HOPS, 2, -1))
 
         @pl.when(t < blocks)
         def _():
-            compute(t)
-            stage(0, t)
+            front(t)
+
+        events(2)
+
+        @pl.when(t == 0)
+        def _():
+            load_wg.wait()
+            load_wu.wait()
+
+        @pl.when(t < blocks)
+        def _():
+            back_half(t, 0)
+
+        events(1, 0)
+
+        @pl.when(t < blocks)
+        def _():
+            stage(0, t, (0, 1))
+            back_half(t, 1)
+            stage(0, t, (2, 3))
 
         @pl.when(t == blocks - 1)
         def _():
@@ -263,9 +257,31 @@
             def _(i):
                 weights(first + i)
 
-    for j in range(slabs - 2, slabs):
-        for copy in store_slab(j, j % 2):
-            copy.wait()
+
+def finish(dx_in, wgu, wd, dx, dw_gate, dw_up, dw_down, buf, in_sem, out_sem, w_sem):
+    ff = wd.shape[0]
+    pieces = dx.shape[0] // BLOCK
+    reads = []
+    for i in range(pieces):
+        r = pl.ds(i * BLOCK, BLOCK)
+        copy = pltpu.make_async_copy(dx_in.at[r, :], buf.at[r, :], in_sem.at[i])
+        copy.start()
+        reads.append(copy)
+    copies = [
+        pltpu.make_async_copy(wgu.at[:, pl.ds(0, ff)], dw_gate, w_sem.at[0]),
+        pltpu.make_async_copy(wgu.at[:, pl.ds(ff, ff)], dw_up, w_sem.at[1]),
+        pltpu.make_async_copy(wd, dw_down, w_sem.at[2]),
+    ]
+    for copy in copies:
+        copy.start()
+    for i, read in enumerate(reads):
+        r = pl.ds(i * BLOCK, BLOCK)
+        read.wait()
+        copy = pltpu.make_async_copy(buf.at[r, :], dx.at[r, :], out_sem.at[i])
+        copy.start()
+        copies.append(copy)
+    for copy in copies:
+        copy.wait()
 
 
 def solution(mesh):
@@ -280,19 +296,17 @@
         quarter = d // 4
         hbm = pl.BlockSpec(memory_space=pl.ANY)
         dma = pltpu.SemaphoreType.DMA
-        return pl.pallas_call(
+        vmem = pl.BlockSpec(memory_space=pltpu.VMEM)
+        dx_raw, dw_gu, dw_d = pl.pallas_call(
             functools.partial(kernel, side),
             out_shape=(
-                jax.ShapeDtypeStruct((rows, d), BF16),
-                jax.ShapeDtypeStruct((d, ff), BF16),
-                jax.ShapeDtypeStruct((d, ff), BF16),
-                jax.ShapeDtypeStruct((ff, d), BF16),
+                pltpu.HBM((rows, d), BF16),
+                pltpu.VMEM((d, 2 * ff), BF16),
+                pltpu.VMEM((ff, d), BF16),
             ),
             in_specs=[hbm] * 7,
-            out_specs=(hbm,) * 4,
+            out_specs=(hbm, vmem, vmem),
             scratch_shapes=[
-                pltpu.VMEM((d, 2 * ff), BF16),
-                pltpu.VMEM((ff, d), BF16),
                 pltpu.VMEM((rows, 2 * ff), BF16),
                 pltpu.VMEM((ff, rows), BF16),
                 pltpu.VMEM((2, BLOCK, d), BF16),
@@ -310,9 +324,6 @@
                 pltpu.VMEM((2, rows, SLAB), BF16),
                 pltpu.VMEM((SLAB, rows), BF16),
                 pltpu.VMEM((2, rows, SLAB), BF16),
-                pltpu.VMEM((2, SLAB, ff), BF16),
-                pltpu.VMEM((2, SLAB, ff), BF16),
-                pltpu.VMEM((2, ff, SLAB), BF16),
                 dma((2, 3)),
                 dma((3,)),
                 dma((HOPS, 4)),
@@ -323,12 +334,31 @@
                 dma((2, 2 * HOPS, 4)),
                 dma((4,)),
                 dma((2, 2)),
-                dma((2, 3)),
             ],
             compiler_params=pltpu.CompilerParams(
-                collective_id=0, has_side_effects=True, vmem_limit_bytes=67043328
+                collective_id=0, has_side_effects=True, vmem_limit_bytes=47_000_000
             ),
         )(x, dy, gate, up, w_gate, w_up, w_down)
+        pieces = rows // BLOCK
+        return pl.pallas_call(
+            finish,
+            out_shape=(
+                jax.ShapeDtypeStruct((rows, d), BF16),
+                jax.ShapeDtypeStruct((d, ff), BF16),
+                jax.ShapeDtypeStruct((d, ff), BF16),
+                jax.ShapeDtypeStruct((ff, d), BF16),
+            ),
+            in_specs=[hbm, vmem, vmem],
+            out_specs=(hbm,) * 4,
+            scratch_shapes=[
+                pltpu.VMEM((rows, d), BF16), dma((pieces,)), dma((pieces,)), dma((3,)),
+            ],
+            compiler_params=pltpu.CompilerParams(vmem_limit_bytes=20_000_000),
+        )(
+            pltpu.with_memory_space_constraint(dx_raw, pltpu.HBM),
+            pltpu.with_memory_space_constraint(dw_gu, pltpu.VMEM),
+            pltpu.with_memory_space_constraint(dw_d, pltpu.VMEM),
+        )
 
     tokens, columns, rows = P("dp", None), P(None, "tp"), P("tp", None)
     return jax.shard_map(

time: 230 us -> 193 us (0.84)
  local copies, waits for them, and re-layouts: 27.2 us -> 0 us
  Pallas kernels: 202 us -> 192 us
    unnamed x10 -> x0, local copies, waits for them, and re-layouts: 27.2 us -> none
    pallas_call x1 -> x2, Pallas kernels: 202 us -> 192 us  [the longest x1 175 us: step(): pl.pallas_call(functools.partial(kernel, side), out_shape=(pltpu.HBM((row...]
where the time goes in v2:
time: 193 us; the launch traced here: 192 us
  Pallas kernels  192 us (99%)
    pallas_call x1, Pallas kernels, step(): pl.pallas_call(functools.partial(kernel, side), out_shape=(pltpu.HBM((row...  175 us
    pallas_call x1, Pallas kernels, step(): pl.pallas_call(finish, out_shape=(jax.ShapeDtypeStruct((rows, d), BF16),...  16.6 us

profile of v2, /device:TPU:96, one launch (start us, length us, event | category | flops | bytes accessed | tf_op | source)
XLA Modules:
  0.0 192.3 jit_solution(4267154008154994842)
XLA Ops:
  0.6 175.0 %shard_map.102 = (bf16[2048,3584]{1,0:T(8,128)(2,1)}, bf16[3584,1792]{1,0:T(8,128)(2,1)S(1)}, bf16[896,3584]{1,0:T(8,128)(2,1)S(1)}) custom-call(bf16[2048,3584]{1,0:T(8,128)(2,1)} %x.1, bf16[2048,3584]{1,0:T(8,128)(2,1)} %dy.1, bf16[2048,896]{1,0:T(8,128)(2,1)} %gate.1, bf16[2048,896]{1,0:T(8,128)(2,1)} %up.1, bf16[3584,896]{1,0:T(8,128)(2,1)} %w_gate.1, ...), custom_call_target="tpu_custom_call" | custom-call | tf_op jit(solution)/shard_map/pallas_call | solution.py:300
  175.7 16.6 %shard_map.103 = (bf16[2048,3584]{1,0:T(8,128)(2,1)}, bf16[3584,896]{1,0:T(8,128)(2,1)}, bf16[3584,896]{1,0:T(8,128)(2,1)}, bf16[896,3584]{1,0:T(8,128)(2,1)}) custom-call(bf16[2048,3584]{1,0:T(8,128)(2,1)} %get-tuple-element.7.dx_in, bf16[3584,1792]{1,0:T(8,128)(2,1)S(1)} %get-tuple-element.8.wgu, bf16[896,3584]{1,0:T(8,128)(2,1)S(1)} %get-tuple-element.9.wd), custom_call_target="tpu_custom_call" | custom-call | tf_op jit(solution)/shard_map/pallas_call | solution.py:343

commit v3 on v2

v3 whole, which is shorter than its diff:
```python
import functools
import math

import jax
import jax.numpy as jnp
from jax import lax
from jax.experimental import pallas as pl
from jax.experimental.pallas import tpu as pltpu
from jax.sharding import PartitionSpec as P

MESH = pl.DeviceIdType.MESH
F32 = jnp.float32
BF16 = jnp.bfloat16
LAST = (((1,), (1,)), ((), ()))

BLOCK = 256
SLAB = 256
ACT_ROWS = 32
CHUNKS = 4
VMEM = 33_090_000
HOPS = 3


def act_back(gate, up, d_hidden):
    k = math.sqrt(2 / math.pi)
    square = gate * gate
    t = jnp.tanh(gate * (k + (k * 0.044715) * square))
    cdf = 0.5 + 0.5 * t
    gelu = gate * cdf
    slope = cdf + (0.5 * gate) * (1 - t * t) * (k + (3 * k * 0.044715) * square)
    return gelu * up, d_hidden * up * slope, d_hidden * gelu


def kernel(
    side, x, dy, gate, up, w_gate, w_up, w_down,
    dx, wgu, wd,
    dgu, hid_t, dh, term, acc, st1, rv1, st2, rv2, xb, xt, yb,
    in_sem, w_sem, s1_send, s2_send, r1_recv, r2_recv, ag_send, ag_recv, xy_sem, chunk_sem,
):
    rows, d = dx.shape
    ff = w_down.shape[0]
    blocks = rows // BLOCK
    part = BLOCK // side
    sub = part // side
    quarter = d // 4
    slabs = d // SLAB

    me = lax.axis_index("tp")
    px, py = me // side, me % side

    def device(axis, sign):
        if axis == 0:
            return {"tp": (px + side + sign) % side * side + py}
        return {"tp": px * side + (py + side + sign) % side}

    flows = ((0, 1, 1), (0, 1, -1), (1, 0, 1), (1, 0, -1))
    pos = (px, py)

    def cols(c):
        return pl.ds(c * quarter, quarter)

    def load_block(t):
        slot = t % 2
        r = pl.ds(pl.multiple_of(t * BLOCK, BLOCK), BLOCK)
        return (
            pltpu.make_async_copy(dy.at[r, :], dx.at[r, :], in_sem.at[slot, 0]),
            pltpu.make_async_copy(gate.at[r, :], dgu.at[r, pl.ds(0, ff)], in_sem.at[slot, 1]),
            pltpu.make_async_copy(up.at[r, :], dgu.at[r, pl.ds(ff, ff)], in_sem.at[slot, 2]),
        )

    def load_half(i):
        n = pl.ds(i * (d // 2), d // 2)
        return (
            pltpu.make_async_copy(w_gate.at[n, :], wgu.at[n, pl.ds(0, ff)], w_sem.at[i, 0]),
            pltpu.make_async_copy(w_up.at[n, :], wgu.at[n, pl.ds(ff, ff)], w_sem.at[i, 1]),
        )

    chunk = d // CHUNKS

    def load_chunk(i):
        n = pl.ds(i * chunk, chunk)
        return (
            pltpu.make_async_copy(w_down.at[:, n], wd.at[:, n], chunk_sem.at[i, 0]),
            pltpu.make_async_copy(dy.at[pl.ds(0, BLOCK), n], dx.at[pl.ds(0, BLOCK), n], chunk_sem.at[i, 1]),
        )

    for i in range(CHUNKS):
        for copy in load_chunk(i):
            copy.start()
    for copy in (*load_block(0)[1:], *load_half(0), *load_half(1)):
        copy.start()

    barrier = pltpu.get_barrier_semaphore()
    for axis in (0, 1):
        for sign in (1, -1):
            pl.semaphore_signal(barrier, inc=1, device_id=device(axis, sign), device_id_type=MESH)
    pl.semaphore_wait(barrier, 4)

    def hop(h, c, b):
        a1, a2, sign = flows[c]
        slot = b % 2
        if h < HOPS:
            return pltpu.make_async_remote_copy(
                st1.at[h, c], rv1.at[slot, h, c], s1_send.at[h, c], r1_recv.at[slot, h, c],
                device_id=device(a1, sign), device_id_type=MESH,
            )
        if h < 2 * HOPS:
            s = h - HOPS
            return pltpu.make_async_remote_copy(
                st2.at[s, c], rv2.at[slot, s, c], s2_send.at[s, c], r2_recv.at[slot, s, c],
                device_id=device(a2, sign), device_id_type=MESH,
            )
        s = h - 2 * HOPS
        p1, p2 = pos[a1], pos[a2]
        if s < HOPS:
            q = (p2 + side - sign * s) % side
            r = pl.ds(pl.multiple_of(b * BLOCK + p1 * part + q * sub, sub), sub)
            to = device(a2, sign)
        else:
            q = (p1 + side - sign * (s - HOPS)) % side
            r = pl.ds(pl.multiple_of(b * BLOCK + q * part, part), part)
            to = device(a1, sign)
        where = dx.at[r, cols(c)]
        return pltpu.make_async_remote_copy(
            where, where, ag_send.at[s, c], ag_recv.at[slot, s, c],
            device_id=to, device_id_type=MESH,
        )

    def term_part(b, c, q):
        r = pl.ds(pl.multiple_of(q * part, part), part)
        return term[b % 2, r, cols(c)]

    def stage(h, b, which=range(4)):
        for c in which:
            a1, a2, sign = flows[c]
            p1, p2 = pos[a1], pos[a2]
            if h > 0:
                hop(h - 1, c, b).wait_recv()
            if h < HOPS:
                q = (p1 + 2 * side - sign * (1 + h)) % side
                value = term_part(b, c, q)
                if h > 0:
                    value = value + rv1[b % 2, h - 1, c].astype(F32)
                st1[h, c] = value.astype(BF16)
                if h == HOPS - 1:
                    acc[b % 4, c] = term_part(b, c, p1)
            elif h < 2 * HOPS:
                s = h - HOPS
                if s == 0:
                    acc[b % 4, c] = acc[b % 4, c] + rv1[b % 2, HOPS - 1, c].astype(F32)
                q = (p2 + 2 * side - sign * (1 + s)) % side
                value = acc[b % 4, c, pl.ds(pl.multiple_of(q * sub, sub), sub), :]
                if s > 0:
                    value = value + rv2[b % 2, s - 1, c].astype(F32)
                st2[s, c] = value.astype(BF16)
            elif h == 2 * HOPS:
                value = acc[b % 4, c, pl.ds(pl.multiple_of(p2 * sub, sub), sub), :]
                r = pl.ds(pl.multiple_of(b * BLOCK + p1 * part + p2 * sub, sub), sub)
                dx[r, cols(c)] = (value + rv2[b % 2, HOPS - 1, c].astype(F32)).astype(BF16)
            if h < 4 * HOPS:
                hop(h, c, b).start()

    def front(t):
        base = pl.multiple_of(t * BLOCK, BLOCK)

        @pl.when(t == 0)
        def _():
            for i in range(CHUNKS):
                n = pl.ds(i * chunk, chunk)
                for copy in load_chunk(i):
                    copy.wait()
                value = lax.dot_general(
                    dx[pl.ds(0, BLOCK), n], wd[:, n], LAST, preferred_element_type=F32
                )
                dh[...] = value if i == 0 else dh[...] + value
            for copy in load_block(0)[1:]:
                copy.wait()

        @pl.when(t > 0)
        def _():
            for copy in load_block(t):
                copy.wait()
            dh[...] = lax.dot_general(
                dx[pl.ds(base, BLOCK), :], wd[...], LAST, preferred_element_type=F32
            )

        @pl.when(t + 1 < blocks)
        def _():
            for copy in load_block(t + 1):
                copy.start()

        @pl.loop(0, BLOCK // ACT_ROWS)
        def _(i):
            r = pl.ds(pl.multiple_of(i * ACT_ROWS, ACT_ROWS), ACT_ROWS)
            g = pl.ds(pl.multiple_of(base + i * ACT_ROWS, ACT_ROWS), ACT_ROWS)
            hidden, d_gate, d_up = act_back(
                dgu[g, pl.ds(0, ff)].astype(F32), dgu[g, pl.ds(ff, ff)].astype(F32), dh[r, :]
            )
            dgu[g, pl.ds(0, ff)] = d_gate.astype(BF16)
            dgu[g, pl.ds(ff, ff)] = d_up.astype(BF16)
            dx[g, pl.ds(0, ff)] = hidden.astype(BF16)

    def back_half(t, i):
        @pl.when(t == 0)
        def _():
            for copy in load_half(i):
                copy.wait()

        lhs = dgu[pl.ds(pl.multiple_of(t * BLOCK, BLOCK), BLOCK), :]
        n = pl.ds(i * (d // 2), d // 2)
        term[t % 2, :, n] = lax.dot_general(lhs, wgu[n, :], LAST, preferred_element_type=F32)

    def keep_hidden(t):
        r = pl.ds(pl.multiple_of(t * BLOCK, BLOCK), BLOCK)
        hid_t[:, r] = dx[r, pl.ds(0, ff)].T

    def load_x(j):
        n = pl.ds(pl.multiple_of(j * SLAB, SLAB), SLAB)
        return pltpu.make_async_copy(x.at[:, n], xb, xy_sem.at[0])

    def load_y(j):
        n = pl.ds(pl.multiple_of(j * SLAB, SLAB), SLAB)
        return pltpu.make_async_copy(dy.at[:, n], yb, xy_sem.at[1])

    def weights(j):
        n = pl.ds(pl.multiple_of(j * SLAB, SLAB), SLAB)
        load_x(j).wait()
        xt[...] = xb[...].T

        @pl.when(j + 1 < slabs)
        def _():
            load_x(j + 1).start()

        for i in range(2):
            f = pl.ds(i * ff, ff)
            wgu[n, f] = jnp.dot(xt[...], dgu[:, f], preferred_element_type=F32).astype(BF16)
        load_y(j).wait()
        wd[:, n] = jnp.dot(hid_t[...], yb[...], preferred_element_type=F32).astype(BF16)

        @pl.when(j + 1 < slabs)
        def _():
            load_y(j + 1).start()

    @pl.loop(0, blocks + 4 * HOPS + 1)
    def _(t):
        def events(*hops, which=range(4)):
            for h in hops:
                b = t - h
                if h < 4 * HOPS:
                    @pl.when((b >= 1) & (b <= blocks))
                    def _():
                        for c in which:
                            hop(h, c, b - 1).wait_send()

                if h > 0:
                    @pl.when((b >= 0) & (b < blocks))
                    def _():
                        stage(h, b, which)

        events(*range(4 * HOPS, 2, -1))

        @pl.when(t < blocks)
        def _():
            front(t)

        events(2)
        events(1, which=(0, 1))

        @pl.when(t < blocks)
        def _():
            back_half(t, 0)

        events(1, which=(2, 3))
        events(0)

        @pl.when(t < blocks)
        def _():
            stage(0, t, (0, 1))
            back_half(t, 1)
            keep_hidden(t)
            stage(0, t, (2, 3))

        @pl.when(t == blocks - 1)
        def _():
            load_x(0).start()
            load_y(0).start()

        first = (t - blocks) * 2

        @pl.when((t >= blocks) & (first < slabs))
        def _():
            @pl.loop(0, 2)
            def _(i):
                weights(first + i)


def finish(dx_in, wgu, wd, dx, dw_gate, dw_up, dw_down, sem):
    ff = wd.shape[0]
    copies = []

    def add(source, target, pieces):
        rows = target.shape[0] // pieces
        for i in range(pieces):
            r = pl.ds(i * rows, rows)
            copy = pltpu.make_async_copy(source(r), target.at[r, :], sem.at[len(copies)])
            copy.start()
            copies.append(copy)

    add(lambda r: dx_in.at[r, :], dx, 8)
    add(lambda r: wgu.at[r, pl.ds(0, ff)], dw_gate, 4)
    add(lambda r: wgu.at[r, pl.ds(ff, ff)], dw_up, 4)
    add(lambda r: wd.at[r, :], dw_down, 4)
    for copy in copies:
        copy.wait()


def solution(mesh):
    n = mesh.shape["tp"]
    side = math.isqrt(n)

    def step(x, dy, gate, up, w_gate, w_up, w_down):
        rows, d = x.shape
        ff = w_down.shape[0]
        part = BLOCK // side
        sub = part // side
        quarter = d // 4
        hbm = pl.BlockSpec(memory_space=pl.ANY)
        dma = pltpu.SemaphoreType.DMA
        vmem = pl.BlockSpec(memory_space=pltpu.VMEM)
        dx_raw, dw_gu, dw_d = pl.pallas_call(
            functools.partial(kernel, side),
            out_shape=(
                pltpu.VMEM((rows, d), BF16),
                pltpu.VMEM((d, 2 * ff), BF16),
                pltpu.VMEM((ff, d), BF16),
            ),
            in_specs=[hbm] * 7,
            out_specs=(vmem,) * 3,
            scratch_shapes=[
                pltpu.VMEM((rows, 2 * ff), BF16),
                pltpu.VMEM((ff, rows), BF16),
                pltpu.VMEM((BLOCK, ff), F32),
                pltpu.VMEM((2, BLOCK, d), F32),
                pltpu.VMEM((4, 4, part, quarter), F32),
                pltpu.VMEM((HOPS, 4, part, quarter), BF16),
                pltpu.VMEM((2, HOPS, 4, part, quarter), BF16),
                pltpu.VMEM((HOPS, 4, sub, quarter), BF16),
                pltpu.VMEM((2, HOPS, 4, sub, quarter), BF16),
                pltpu.VMEM((rows, SLAB), BF16),
                pltpu.VMEM((SLAB, rows), BF16),
                pltpu.VMEM((rows, SLAB), BF16),
                dma((2, 3)),
                dma((2, 2)),
                dma((HOPS, 4)),
                dma((HOPS, 4)),
                dma((2, HOPS, 4)),
                dma((2, HOPS, 4)),
                dma((2 * HOPS, 4)),
                dma((2, 2 * HOPS, 4)),
                dma((2,)),
                dma((CHUNKS, 2)),
            ],
            compiler_params=pltpu.CompilerParams(
                collective_id=0, has_side_effects=True, vmem_limit_bytes=VMEM
            ),
        )(x, dy, gate, up, w_gate, w_up, w_down)
        return pl.pallas_call(
            finish,
            out_shape=(
                jax.ShapeDtypeStruct((rows, d), BF16),
                jax.ShapeDtypeStruct((d, ff), BF16),
                jax.ShapeDtypeStruct((d, ff), BF16),
                jax.ShapeDtypeStruct((ff, d), BF16),
            ),
            in_specs=[vmem] * 3,
            out_specs=(hbm,) * 4,
            scratch_shapes=[dma((20,))],
            compiler_params=pltpu.CompilerParams(vmem_limit_bytes=VMEM),
        )(
            pltpu.with_memory_space_constraint(dx_raw, pltpu.VMEM),
            pltpu.with_memory_space_constraint(dw_gu, pltpu.VMEM),
            pltpu.with_memory_space_constraint(dw_d, pltpu.VMEM),
        )

    tokens, columns, rows = P("dp", None), P(None, "tp"), P("tp", None)
    return jax.shard_map(
        step,
        mesh=mesh,
        in_specs=(tokens, tokens, P("dp", "tp"), P("dp", "tp"), columns, columns, rows),
        out_specs=(tokens, P("dp", "tp"), P("dp", "tp"), P(("dp", "tp"), None)),
        check_vma=False,
    )
```

time: 193 us -> 187 us (0.969)
  Pallas kernels: 192 us -> 186 us
    pallas_call x1, Pallas kernels: 16.6 us -> 11.2 us  [step(): pl.pallas_call(finish, out_shape=(jax.ShapeDtypeStruct((rows, d), BF16),...]
where the time goes in v3:
time: 187 us; the launch traced here: 186 us
  Pallas kernels  186 us (99%)
    pallas_call x1, Pallas kernels, step(): pl.pallas_call(functools.partial(kernel, side), out_shape=(pltpu.VMEM((ro...  174 us
    pallas_call x1, Pallas kernels, step(): pl.pallas_call(finish, out_shape=(jax.ShapeDtypeStruct((rows, d), BF16),...  11.2 us

profile of v3, /device:TPU:96, one launch (start us, length us, event | category | flops | bytes accessed | tf_op | source)
XLA Modules:
  0.0 186.4 jit_solution(14258367512215713655)
XLA Ops:
  0.6 174.5 %shard_map.102 = (bf16[2048,3584]{1,0:T(8,128)(2,1)S(1)}, bf16[3584,1792]{1,0:T(8,128)(2,1)S(1)}, bf16[896,3584]{1,0:T(8,128)(2,1)S(1)}) custom-call(bf16[2048,3584]{1,0:T(8,128)(2,1)} %x.1, bf16[2048,3584]{1,0:T(8,128)(2,1)} %dy.1, bf16[2048,896]{1,0:T(8,128)(2,1)} %gate.1, bf16[2048,896]{1,0:T(8,128)(2,1)} %up.1, bf16[3584,896]{1,0:T(8,128)(2,1)} %w_gate.1, ...), custom_call_target="tpu_custom_call" | custom-call | tf_op jit(solution)/shard_map/pallas_call | solution.py:330
  175.1 11.2 %shard_map.103 = (bf16[2048,3584]{1,0:T(8,128)(2,1)}, bf16[3584,896]{1,0:T(8,128)(2,1)}, bf16[3584,896]{1,0:T(8,128)(2,1)}, bf16[896,3584]{1,0:T(8,128)(2,1)}) custom-call(bf16[2048,3584]{1,0:T(8,128)(2,1)S(1)} %get-tuple-element.7.dx_in, bf16[3584,1792]{1,0:T(8,128)(2,1)S(1)} %get-tuple-element.8.wgu, bf16[896,3584]{1,0:T(8,128)(2,1)S(1)} %get-tuple-element.9.wd), custom_call_target="tpu_custom_call" | custom-call | tf_op jit(solution)/shard_map/pallas_call | solution.py:367

commit v4 on v3

--- a/solution.py
+++ b/solution.py
@@ -17,6 +17,7 @@
 SLAB = 256
 ACT_ROWS = 32
 CHUNKS = 4
+STARTS = (1, 3)
 VMEM = 33_090_000
 HOPS = 3
 
@@ -87,7 +88,7 @@
     for i in range(CHUNKS):
         for copy in load_chunk(i):
             copy.start()
-    for copy in (*load_block(0)[1:], *load_half(0), *load_half(1)):
+    for copy in load_block(0)[1:]:
         copy.start()
 
     barrier = pltpu.get_barrier_semaphore()
@@ -169,6 +170,9 @@
                 n = pl.ds(i * chunk, chunk)
                 for copy in load_chunk(i):
                     copy.wait()
+                if i in STARTS:
+                    for copy in load_half(STARTS.index(i)):
+                        copy.start()
                 value = lax.dot_general(
                     dx[pl.ds(0, BLOCK), n], wd[:, n], LAST, preferred_element_type=F32
                 )
@@ -257,7 +261,14 @@
                     def _():
                         stage(h, b, which)
 
-        events(*range(4 * HOPS, 2, -1))
+        events(*range(4 * HOPS, 3 * HOPS, -1))
+        first = (t - blocks) * 2
+
+        @pl.when((t >= blocks) & (first < slabs))
+        def _():
+            weights(first)
+
+        events(*range(3 * HOPS, 2, -1))
 
         @pl.when(t < blocks)
         def _():
@@ -285,13 +296,9 @@
             load_x(0).start()
             load_y(0).start()
 
-        first = (t - blocks) * 2
-
         @pl.when((t >= blocks) & (first < slabs))
         def _():
-            @pl.loop(0, 2)
-            def _(i):
-                weights(first + i)
+            weights(first + 1)
 
 
 def finish(dx_in, wgu, wd, dx, dw_gate, dw_up, dw_down, sem):

time: 187 us -> 184 us (0.984)
  Pallas kernels: 186 us -> 184 us
    pallas_call x1, Pallas kernels: 174 us -> 172 us  [step(): pl.pallas_call(functools.partial(kernel, side), out_shape=(pltpu.VMEM((ro...]
where the time goes in v4:
time: 184 us
  Pallas kernels  184 us (100%)
    pallas_call x1, Pallas kernels, step(): pl.pallas_call(functools.partial(kernel, side), out_shape=(pltpu.VMEM((ro...  172 us
    pallas_call x1, Pallas kernels, step(): pl.pallas_call(finish, out_shape=(jax.ShapeDtypeStruct((rows, d), BF16),...  11.2 us

profile of v4, /device:TPU:96, one launch (start us, length us, event | category | flops | bytes accessed | tf_op | source)
XLA Modules:
  0.0 184.2 jit_solution(17941323690723321688)
XLA Ops:
  0.6 172.4 %shard_map.102 = (bf16[2048,3584]{1,0:T(8,128)(2,1)S(1)}, bf16[3584,1792]{1,0:T(8,128)(2,1)S(1)}, bf16[896,3584]{1,0:T(8,128)(2,1)S(1)}) custom-call(bf16[2048,3584]{1,0:T(8,128)(2,1)} %x.1, bf16[2048,3584]{1,0:T(8,128)(2,1)} %dy.1, bf16[2048,896]{1,0:T(8,128)(2,1)} %gate.1, bf16[2048,896]{1,0:T(8,128)(2,1)} %up.1, bf16[3584,896]{1,0:T(8,128)(2,1)} %w_gate.1, ...), custom_call_target="tpu_custom_call" | custom-call | tf_op jit(solution)/shard_map/pallas_call | solution.py:337
  173.0 11.2 %shard_map.103 = (bf16[2048,3584]{1,0:T(8,128)(2,1)}, bf16[3584,896]{1,0:T(8,128)(2,1)}, bf16[3584,896]{1,0:T(8,128)(2,1)}, bf16[896,3584]{1,0:T(8,128)(2,1)}) custom-call(bf16[2048,3584]{1,0:T(8,128)(2,1)S(1)} %get-tuple-element.7.dx_in, bf16[3584,1792]{1,0:T(8,128)(2,1)S(1)} %get-tuple-element.8.wgu, bf16[896,3584]{1,0:T(8,128)(2,1)S(1)} %get-tuple-element.9.wd), custom_call_target="tpu_custom_call" | custom-call | tf_op jit(solution)/shard_map/pallas_call | solution.py:374

commit v5 on v4

--- a/solution.py
+++ b/solution.py
@@ -19,7 +19,11 @@
 CHUNKS = 4
 STARTS = (1, 3)
 VMEM = 33_090_000
-HOPS = 3
+RING = 3
+SCATTER = 2
+GATHER = SCATTER + RING
+LAST_GATHER = GATHER + RING
+ALL = LAST_GATHER + 2
 
 
 def act_back(gate, up, d_hidden):
@@ -35,7 +39,7 @@
 def kernel(
     side, x, dy, gate, up, w_gate, w_up, w_down,
     dx, wgu, wd,
-    dgu, hid_t, dh, term, acc, st1, rv1, st2, rv2, xb, xt, yb,
+    dgu, hid_t, dh, term, acc, st1, rv1, rvx, st2, rv2, xb, xt, yb,
     in_sem, w_sem, s1_send, s2_send, r1_recv, r2_recv, ag_send, ag_recv, xy_sem, chunk_sem,
 ):
     rows, d = dx.shape
@@ -100,66 +104,84 @@
     def hop(h, c, b):
         a1, a2, sign = flows[c]
         slot = b % 2
-        if h < HOPS:
-            return pltpu.make_async_remote_copy(
-                st1.at[h, c], rv1.at[slot, h, c], s1_send.at[h, c], r1_recv.at[slot, h, c],
-                device_id=device(a1, sign), device_id_type=MESH,
-            )
-        if h < 2 * HOPS:
-            s = h - HOPS
-            return pltpu.make_async_remote_copy(
+        p1, p2 = pos[a1], pos[a2]
+        if h < SCATTER:
+            made = []
+            for k in (0, 1) if h == 0 else (2,):
+                late = b % 3 if k == 1 else slot
+                made.append(pltpu.make_async_remote_copy(
+                    st1.at[k, c], rvx.at[late, c] if k == 1 else rv1.at[slot, k // 2, c],
+                    s1_send.at[k, c], r1_recv.at[late, k, c],
+                    device_id=device(a1, sign), device_id_type=MESH,
+                ))
+            return made
+        if h < GATHER:
+            s = h - SCATTER
+            return [pltpu.make_async_remote_copy(
                 st2.at[s, c], rv2.at[slot, s, c], s2_send.at[s, c], r2_recv.at[slot, s, c],
                 device_id=device(a2, sign), device_id_type=MESH,
-            )
-        s = h - 2 * HOPS
-        p1, p2 = pos[a1], pos[a2]
-        if s < HOPS:
+            )]
+        s = h - GATHER
+        n = cols(c)
+        if h < LAST_GATHER:
             q = (p2 + side - sign * s) % side
             r = pl.ds(pl.multiple_of(b * BLOCK + p1 * part + q * sub, sub), sub)
             to = device(a2, sign)
         else:
-            q = (p1 + side - sign * (s - HOPS)) % side
+            q = p1
+            if h == LAST_GATHER:
+                n = pl.ds(c // 2 * 2 * quarter, 2 * quarter)
+            else:
+                q = (p1 + side - sign) % side
             r = pl.ds(pl.multiple_of(b * BLOCK + q * part, part), part)
             to = device(a1, sign)
-        where = dx.at[r, cols(c)]
-        return pltpu.make_async_remote_copy(
+        where = dx.at[r, n]
+        return [pltpu.make_async_remote_copy(
             where, where, ag_send.at[s, c], ag_recv.at[slot, s, c],
             device_id=to, device_id_type=MESH,
-        )
+        )]
 
     def term_part(b, c, q):
         r = pl.ds(pl.multiple_of(q * part, part), part)
         return term[b % 2, r, cols(c)]
 
     def stage(h, b, which=range(4)):
+        if h in (SCATTER, LAST_GATHER):
+            for c in which:
+                hop(h - 1, c, b)[0].wait_recv()
+                if h == SCATTER:
+                    hop(0, c, b)[1].wait_recv()
         for c in which:
             a1, a2, sign = flows[c]
             p1, p2 = pos[a1], pos[a2]
-            if h > 0:
-                hop(h - 1, c, b).wait_recv()
-            if h < HOPS:
-                q = (p1 + 2 * side - sign * (1 + h)) % side
-                value = term_part(b, c, q)
-                if h > 0:
-                    value = value + rv1[b % 2, h - 1, c].astype(F32)
-                st1[h, c] = value.astype(BF16)
-                if h == HOPS - 1:
-                    acc[b % 4, c] = term_part(b, c, p1)
-            elif h < 2 * HOPS:
-                s = h - HOPS
+            if h not in (0, SCATTER, LAST_GATHER):
+                hop(h - 1, c, b)[0].wait_recv()
+            near = (p1 + side + sign) % side
+            if h == 0:
+                st1[0, c] = term_part(b, c, (p1 + side + 2 * sign) % side).astype(BF16)
+                st1[1, c] = term_part(b, c ^ 1, near).astype(BF16)
+            elif h == 1:
+                st1[2, c] = (term_part(b, c, near) + rv1[b % 2, 0, c].astype(F32)).astype(BF16)
+            elif h < GATHER:
+                s = h - SCATTER
                 if s == 0:
-                    acc[b % 4, c] = acc[b % 4, c] + rv1[b % 2, HOPS - 1, c].astype(F32)
+                    acc[b % 3, c] = (
+                        term_part(b, c, p1)
+                        + rv1[b % 2, 1, c].astype(F32)
+                        + rvx[b % 3, c ^ 1].astype(F32)
+                    )
                 q = (p2 + 2 * side - sign * (1 + s)) % side
-                value = acc[b % 4, c, pl.ds(pl.multiple_of(q * sub, sub), sub), :]
+                value = acc[b % 3, c, pl.ds(pl.multiple_of(q * sub, sub), sub), :]
                 if s > 0:
                     value = value + rv2[b % 2, s - 1, c].astype(F32)
                 st2[s, c] = value.astype(BF16)
-            elif h == 2 * HOPS:
-                value = acc[b % 4, c, pl.ds(pl.multiple_of(p2 * sub, sub), sub), :]
+            elif h == GATHER:
+                value = acc[b % 3, c, pl.ds(pl.multiple_of(p2 * sub, sub), sub), :]
                 r = pl.ds(pl.multiple_of(b * BLOCK + p1 * part + p2 * sub, sub), sub)
-                dx[r, cols(c)] = (value + rv2[b % 2, HOPS - 1, c].astype(F32)).astype(BF16)
-            if h < 4 * HOPS:
-                hop(h, c, b).start()
+                dx[r, cols(c)] = (value + rv2[b % 2, RING - 1, c].astype(F32)).astype(BF16)
+            if h < ALL:
+                for copy in hop(h, c, b):
+                    copy.start()
 
     def front(t):
         base = pl.multiple_of(t * BLOCK, BLOCK)
@@ -245,36 +267,37 @@
         def _():
             load_y(j + 1).start()
 
-    @pl.loop(0, blocks + 4 * HOPS + 1)
+    @pl.loop(0, blocks + ALL)
     def _(t):
         def events(*hops, which=range(4)):
             for h in hops:
                 b = t - h
-                if h < 4 * HOPS:
+                if h < ALL:
                     @pl.when((b >= 1) & (b <= blocks))
                     def _():
                         for c in which:
-                            hop(h, c, b - 1).wait_send()
+                            for copy in hop(h, c, b - 1):
+                                copy.wait_send()
 
                 if h > 0:
                     @pl.when((b >= 0) & (b < blocks))
                     def _():
                         stage(h, b, which)
 
-        events(*range(4 * HOPS, 3 * HOPS, -1))
+        events(*range(ALL, LAST_GATHER - 1, -1))
         first = (t - blocks) * 2
 
         @pl.when((t >= blocks) & (first < slabs))
         def _():
             weights(first)
 
-        events(*range(3 * HOPS, 2, -1))
+        events(*range(LAST_GATHER - 1, SCATTER, -1))
 
         @pl.when(t < blocks)
         def _():
             front(t)
 
-        events(2)
+        events(SCATTER)
         events(1, which=(0, 1))
 
         @pl.when(t < blocks)
@@ -348,22 +371,23 @@
                 pltpu.VMEM((ff, rows), BF16),
                 pltpu.VMEM((BLOCK, ff), F32),
                 pltpu.VMEM((2, BLOCK, d), F32),
-                pltpu.VMEM((4, 4, part, quarter), F32),
-                pltpu.VMEM((HOPS, 4, part, quarter), BF16),
-                pltpu.VMEM((2, HOPS, 4, part, quarter), BF16),
-                pltpu.VMEM((HOPS, 4, sub, quarter), BF16),
-                pltpu.VMEM((2, HOPS, 4, sub, quarter), BF16),
+                pltpu.VMEM((3, 4, part, quarter), F32),
+                pltpu.VMEM((3, 4, part, quarter), BF16),
+                pltpu.VMEM((2, 2, 4, part, quarter), BF16),
+                pltpu.VMEM((3, 4, part, quarter), BF16),
+                pltpu.VMEM((RING, 4, sub, quarter), BF16),
+                pltpu.VMEM((2, RING, 4, sub, quarter), BF16),
                 pltpu.VMEM((rows, SLAB), BF16),
                 pltpu.VMEM((SLAB, rows), BF16),
                 pltpu.VMEM((rows, SLAB), BF16),
                 dma((2, 3)),
                 dma((2, 2)),
-                dma((HOPS, 4)),
-                dma((HOPS, 4)),
-                dma((2, HOPS, 4)),
-                dma((2, HOPS, 4)),
-                dma((2 * HOPS, 4)),
-                dma((2, 2 * HOPS, 4)),
+                dma((3, 4)),
+                dma((RING, 4)),
+                dma((3, 3, 4)),
+                dma((2, RING, 4)),
+                dma((RING + 2, 4)),
+                dma((2, RING + 2, 4)),
                 dma((2,)),
                 dma((CHUNKS, 2)),
             ],

time: 184 us -> 180 us (0.978)
  Pallas kernels: 184 us -> 179 us
    pallas_call x1, Pallas kernels: 172 us -> 168 us  [step(): pl.pallas_call(functools.partial(kernel, side), out_shape=(pltpu.VMEM((ro...]
where the time goes in v5:
time: 180 us
  Pallas kernels  179 us (99%)
    pallas_call x1, Pallas kernels, step(): pl.pallas_call(functools.partial(kernel, side), out_shape=(pltpu.VMEM((ro...  168 us
    pallas_call x1, Pallas kernels, step(): pl.pallas_call(finish, out_shape=(jax.ShapeDtypeStruct((rows, d), BF16),...  11.2 us

profile of v5, /device:TPU:96, one launch (start us, length us, event | category | flops | bytes accessed | tf_op | source)
XLA Modules:
  0.0 179.6 jit_solution(14305834883279778605)
XLA Ops:
  0.6 167.8 %shard_map.102 = (bf16[2048,3584]{1,0:T(8,128)(2,1)S(1)}, bf16[3584,1792]{1,0:T(8,128)(2,1)S(1)}, bf16[896,3584]{1,0:T(8,128)(2,1)S(1)}) custom-call(bf16[2048,3584]{1,0:T(8,128)(2,1)} %x.1, bf16[2048,3584]{1,0:T(8,128)(2,1)} %dy.1, bf16[2048,896]{1,0:T(8,128)(2,1)} %gate.1, bf16[2048,896]{1,0:T(8,128)(2,1)} %up.1, bf16[3584,896]{1,0:T(8,128)(2,1)} %w_gate.1, ...), custom_call_target="tpu_custom_call" | custom-call | tf_op jit(solution)/shard_map/pallas_call | solution.py:360
  168.4 11.2 %shard_map.103 = (bf16[2048,3584]{1,0:T(8,128)(2,1)}, bf16[3584,896]{1,0:T(8,128)(2,1)}, bf16[3584,896]{1,0:T(8,128)(2,1)}, bf16[896,3584]{1,0:T(8,128)(2,1)}) custom-call(bf16[2048,3584]{1,0:T(8,128)(2,1)S(1)} %get-tuple-element.7.dx_in, bf16[3584,1792]{1,0:T(8,128)(2,1)S(1)} %get-tuple-element.8.wgu, bf16[896,3584]{1,0:T(8,128)(2,1)S(1)} %get-tuple-element.9.wd), custom_call_target="tpu_custom_call" | custom-call | tf_op jit(solution)/shard_map/pallas_call | solution.py:398
